TPU v7x, 32 devices: a whole 2x2x4 slice. The times are simulated.
32 devices in a mesh: tm: 16 (over z, y, core), asset: 2 (over x).
Axes of the slice: x: 2, y: 2, z: 4, core: 2. Of those that a mesh axis runs over, the one named last changes fastest.
Arguments:
- tick_bars: float32 [2, 16, 61440], P('asset', 'tm'), may hold values from -20 to 20
- prior_bars: float32 [2, 16, 6400], P('asset', 'tm'), may hold values from -20 to 20, as said below
Outputs:
- connectedness: float32 [48, 8192], P('tm', 'asset')
Inputs may be any that keep to these rules, and one draw needn't show every extreme that they name: `prior_bars`: bar returns of the same assets.
All inputs are finite; a program needn't handle non-finite values.
Results may differ from a plain program's by a relative error of at most 0.0014.
Values may be sent and summed in bfloat16 or wider, within the bound.
A program may use at most 64 MiB of HBM per device.

v0:
```python
import math

import jax
import jax.numpy as jnp
from jax import lax
from jax.sharding import PartitionSpec as P

ASSETS = 8192
SPAN = 30
STRIDE = 5
WIN_DEV = 3
LEAD = 25


FLOOR_SQUARES = 1.0


def from_behind(x, axis, by):
    size = lax.axis_size(axis)
    pairs = [(i, i + by) for i in range(size) if 0 <= i + by < size]
    return lax.ppermute(x, axis, pairs)


def swapped(block, axis, distance):
    count = lax.axis_size(axis)
    route = []
    for low in range(count):
        high = low | 1 << distance
        if high != low and high < count:
            route += [(low, high), (high, low)]
    return lax.ppermute(block, axis, route)


def window_stack(extended):
    columns = extended.shape[1]
    groups = extended.reshape(-1, STRIDE, columns)
    stacked = jnp.stack(
        [groups[offset : offset + WIN_DEV] for offset in range(SPAN // STRIDE)], axis=1
    )
    values = stacked.reshape(WIN_DEV, SPAN, columns)
    centred = values - jnp.mean(values, axis=1, keepdims=True)
    squares = jnp.sum(centred * centred, axis=1, keepdims=True)
    return (centred * lax.rsqrt(jnp.maximum(squares, FLOOR_SQUARES))).astype(jnp.bfloat16)


def block_magnitude(left_part, right_part, offset, block_rows):
    correlation = lax.dot_general(
        left_part[:, offset : offset + block_rows],
        right_part,
        (((0,), (0,)), ((), ())),
        preferred_element_type=jnp.float32,
    )
    return jnp.abs(correlation.astype(jnp.bfloat16)).astype(jnp.float32)


def row_totals(own_windows, other_windows):
    columns = own_windows.shape[2]
    block_rows = min(1024, columns)

    def row_one_window(operands):
        left_part, right_part = operands
        pieces = [
            jnp.sum(block_magnitude(left_part, right_part, offset, block_rows), axis=1)
            for offset in range(0, columns, block_rows)
        ]
        return jnp.concatenate(pieces)

    return lax.map(row_one_window, (own_windows, other_windows))


def both_totals(own_windows, other_windows):
    columns = own_windows.shape[2]
    block_rows = min(1024, columns)

    def both_one_window(operands):
        left_part, right_part = operands
        pieces = []
        column_total = jnp.zeros((right_part.shape[1],), jnp.float32)
        for offset in range(0, columns, block_rows):
            magnitude = block_magnitude(left_part, right_part, offset, block_rows)
            pieces.append(jnp.sum(magnitude, axis=1))
            column_total = column_total + jnp.sum(magnitude, axis=0)
        return (jnp.concatenate(pieces), column_total)

    return lax.map(both_one_window, (own_windows, other_windows))


def earlier_rows(tail_rows, distance):
    return from_behind(tail_rows, "tm", distance)


def time_block_rows(tick_bars, prior_bars):
    groups = lax.axis_size("tm")
    group_cols = ASSETS // (2 * groups)
    outgoing = tick_bars.reshape(groups, 1, -1)
    arrived = lax.all_to_all(outgoing, "tm", split_axis=0, concat_axis=1, tiled=True)
    block_len = arrived.shape[2] // group_cols
    own_rows = jnp.transpose(arrived.reshape(groups, block_len, group_cols), (1, 0, 2)).reshape(
        block_len, groups * group_cols
    )
    prior_all = lax.all_gather(prior_bars, "tm", axis=1, tiled=True)
    series_prior = jnp.transpose(prior_all.reshape(groups, LEAD, group_cols), (1, 0, 2)).reshape(
        LEAD, groups * group_cols
    )
    reach = (LEAD + block_len - 1) // block_len
    earlier = []
    for distance in range(reach, 0, -1):
        needed = min(block_len, LEAD - (distance - 1) * block_len)
        earlier.append(earlier_rows(own_rows[block_len - needed :], distance))
    history = jnp.concatenate(earlier, axis=0)
    position = lax.axis_index("tm")
    first_row = position * block_len
    padded = jnp.concatenate([series_prior, jnp.zeros_like(series_prior)], axis=0)
    from_prior = lax.dynamic_slice_in_dim(padded, jnp.minimum(first_row, LEAD), LEAD, 0)
    before_start = first_row - LEAD + jnp.arange(LEAD, dtype=jnp.int32) < 0
    history = jnp.where(before_start[:, None], from_prior, history)
    return jnp.concatenate([history, own_rows], axis=0)


def shards(tick_bars, prior_bars):
    extended = time_block_rows(tick_bars, prior_bars)
    scaled = window_stack(extended)
    columns = scaled.shape[2]
    empty = jnp.zeros((WIN_DEV, columns), jnp.float32)
    partner = swapped(scaled, "asset", 0)
    tile_index = lax.axis_index("asset")
    quarter = columns // 2
    diagonal_part = row_totals(scaled, scaled)
    column_part = empty
    cross_rows = []
    for half_index in range(2):
        mine = scaled[:, :, half_index * quarter : (half_index + 1) * quarter]
        target = (half_index + tile_index) % 2
        theirs = lax.dynamic_slice_in_dim(partner, target * quarter, quarter, 2)
        row_add, column_add = both_totals(mine, theirs)
        cross_rows.append(row_add)
        column_part = lax.dynamic_update_slice_in_dim(column_part, column_add, target * quarter, 1)
    returned = swapped(column_part.astype(jnp.bfloat16), "asset", 0).astype(column_part.dtype)
    totals = diagonal_part + jnp.concatenate(cross_rows, axis=1) + returned
    return totals * (math.sqrt(SPAN) / ASSETS)


def solution(mesh):
    in_specs = (P("asset", "tm", None), P("asset", "tm", None))
    out_specs = P("tm", "asset")
    return jax.shard_map(shards, mesh=mesh, in_specs=in_specs, out_specs=out_specs, check_vma=False)
```

profile of v0, /device:TPU:0, one launch (start us, length us, event | category | flops | bytes accessed | tf_op | source)
XLA Modules:
  0.0 132.5 jit_solution(15997069284028944891)
XLA Ops:
  0.0 7.5 %all-to-all-start = ((f32[16,1,3840]{2,1,0:T(1,128)}), f32[16,1,3840]{2,1,0:T(1,128)S(1)}, u32[]{:S(2)}, u32[]{:S(2)}) async-start(f32[16,1,3840]{2,1,0:T(1,128)} %bitcast.93), calls=%async_computation | async-start | bytes 491520 | tf_op jit(solution)/shard_map/all_to_all | solution.py:96
  7.6 9.8 %all-to-all-done = f32[16,1,3840]{2,1,0:T(1,128)S(1)} async-done(((f32[16,1,3840]{2,1,0:T(1,128)}), f32[16,1,3840]{2,1,0:T(1,128)S(1)}, u32[]{:S(2)}, u32[]{:S(2)}) %all-to-all-start) | async-done | bytes 245792 | tf_op jit(solution)/shard_map/all_to_all | solution.py:96
  18.3 1.8 %collective-permute-start.1 = (f32[15,4096]{1,0:T(8,128)S(1)}, f32[15,4096]{1,0:T(8,128)S(1)}, u32[]{:S(2)}, u32[]{:S(2)}) collective-permute-start(f32[15,4096]{1,0:T(8,128)S(1)} %bitcast.86), channel_id=1, source_target_pairs={{0,2},{2,4},{4,6},{6,8},{8,10},{10,12},{12,14},{14,16},{16,18},{18... | collective-permute-start | bytes 737288 | tf_op jit(solution)/shard_map/ppermute | solution.py:21
  20.4 2.5 %collective-permute-start = (f32[10,4096]{1,0:T(8,128)S(1)}, f32[10,4096]{1,0:T(8,128)S(1)}, u32[]{:S(2)}, u32[]{:S(2)}) collective-permute-start(f32[10,4096]{1,0:T(8,128)S(1)} %bitcast.92), channel_id=1, source_target_pairs={{0,4},{2,6},{4,8},{6,10},{8,12},{10,14},{12,16},{14,18},{16,20},{1... | collective-permute-start | bytes 491528 | tf_op jit(solution)/shard_map/ppermute | solution.py:21
  23.0 22.3 %all_gather.3 = f32[1,16,6400]{2,0,1:T(1,128)S(1)} all-gather(f32[1,1,6400]{2,0,1:T(1,128)S(1)} %bitcast.94), channel_id=1, replica_groups=mesh['tm'=16,'asset'=2] {'tm'}, dimensions={1}, use_global_device_ids=true | all-gather | bytes 435200 | tf_op jit(solution)/shard_map/all_gather | solution.py:101
  49.1 1.7 %stack.22 = f32[3,1,5,4096]{3,2,0,1:T(8,128)} reshape(f32[15,4096]{1,0:T(8,128)} %get-tuple-element.124) | data formatting | bytes 491520 | tf_op jit(solution)/shard_map/stack | solution.py:37
  50.8 1.7 %stack.23 = f32[3,1,5,4096]{3,2,0,1:T(8,128)} reshape(f32[15,4096]{1,0:T(8,128)} %get-tuple-element.123) | data formatting | bytes 491520 | tf_op jit(solution)/shard_map/stack | solution.py:37
  57.3 1.6 %copy.14 = f32[3,6,5,4096]{3,2,1,0:T(8,128)} copy(f32[3,6,5,4096]{3,2,0,1:T(8,128)S(1)} %get-tuple-element.137) | data formatting | bytes 2949120 | tf_op jit(solution)/shard_map/stack | solution.py:37
  59.4 1.7 %reshape.86 = f32[3,30,4096]{2,1,0:T(8,128)S(1)} reshape(f32[3,6,5,4096]{3,2,1,0:T(8,128)} %copy.14) | data formatting | bytes 2949120 | tf_op jit(solution)/shard_map/reshape | solution.py:40
  61.3 1.6 %collective-permute-start.2 = (bf16[3,30,4096]{2,1,0:T(8,128)(2,1)S(1)}, bf16[3,30,4096]{2,1,0:T(8,128)(2,1)S(1)}, u32[]{:S(2)}, u32[]{:S(2)}) collective-permute-start(bf16[3,30,4096]{2,1,0:T(8,128)(2,1)S(1)} %multiply_convert_fusion), channel_id=1, source_target_pairs={{0,1},{1,0},{2,3},{3,2},{4,5},{5,4},{6,7},{7,6},{8,9},{9,8},{10,11... | collective-permute-start | bytes 2211848 | tf_op jit(solution)/shard_map/ppermute | solution.py:31
  62.9 18.2 %collective-permute-done.2 = bf16[3,30,4096]{2,1,0:T(8,128)(2,1)S(1)} collective-permute-done((bf16[3,30,4096]{2,1,0:T(8,128)(2,1)S(1)}, bf16[3,30,4096]{2,1,0:T(8,128)(2,1)S(1)}, u32[]{:S(2)}, u32[]{:S(2)}) %collective-permute-start.2) | collective-permute-done | bytes 737312 | tf_op jit(solution)/shard_map/ppermute | solution.py:31
  81.3 9.1 %while.35 = (s32[]{:T(128)}, f32[3,2048]{1,0:T(4,128)S(1)}, f32[3,2048]{1,0:T(4,128)S(1)}, bf16[3,30,2048]{2,1,0:T(8,128)(2,1)S(1)}, bf16[3,30,2048]{2,1,0:T(8,128)(2,1)S(1)}, /*index=5*/s32[]{:T(128)}, s32[]{:T(128)}) while((s32[]{:T(128)}, f32[3,2048]{1,0:T(4,128)S(1)}, f32[3,2048]{1,0:T(4,128)S(1)}, bf16[3,30,2048]{2,1,0:T(8,128)(2,1)S(1)}, ...), condition=%wide.region_18.19_spmd, body=%wide.region_13.18_spmd.sunk | while | flops 272627712 | bytes 737377 | solution.py:85
  82.7 1.4 %convert_reduce_fusion.24 = (f32[2048]{0:T(1024)S(1)}, f32[1024]{0:T(1024)S(1)}) fusion(bf16[3,30,2048]{2,1,0:T(8,128)(2,1)S(1)} %get-tuple-element.289, s32[]{:T(128)} %get-tuple-element.278, bf16[30,2048]{1,0:T(8,128)(2,1)S(1)} %dynamic-slice_bitcast_fusion.7), kind=kOutput, calls=%fused_computation.10.clone.1 | convolution fusion | flops 136311808 | bytes 208900 | tf_op jit(solution)/shard_map/while/body/eval_jaxpr/dot_general | solution.py:47
  87.4 1.4 %convert_reduce_fusion.25 = (f32[2048]{0:T(1024)S(1)}, f32[1024]{0:T(1024)S(1)}) fusion(bf16[3,30,2048]{2,1,0:T(8,128)(2,1)S(1)} %get-tuple-element.289, s32[]{:T(128)} %get-tuple-element.278, bf16[30,2048]{1,0:T(8,128)(2,1)S(1)} %dynamic-slice_bitcast_fusion.7), kind=kOutput, calls=%fused_computation.12.clone.1 | convolution fusion | flops 136311808 | bytes 208900 | tf_op jit(solution)/shard_map/while/body/eval_jaxpr/dot_general | solution.py:47
  90.4 9.2 %while.36 = (s32[]{:T(128)}, f32[3,2048]{1,0:T(4,128)S(1)}, f32[3,2048]{1,0:T(4,128)S(1)}, bf16[3,30,2048]{2,1,0:T(8,128)(2,1)S(1)}, bf16[3,30,2048]{2,1,0:T(8,128)(2,1)S(1)}, /*index=5*/s32[]{:T(128)}, s32[]{:T(128)}) while((s32[]{:T(128)}, f32[3,2048]{1,0:T(4,128)S(1)}, f32[3,2048]{1,0:T(4,128)S(1)}, bf16[3,30,2048]{2,1,0:T(8,128)(2,1)S(1)}, ...), condition=%wide.region_24.25_spmd, body=%wide.region_19.24_spmd.sunk | while | flops 272627712 | bytes 737377 | solution.py:85
  90.5 1.4 %convert_reduce_fusion.27 = (f32[2048]{0:T(1024)S(1)}, f32[1024]{0:T(1024)S(1)}) fusion(bf16[3,30,2048]{2,1,0:T(8,128)(2,1)S(1)} %get-tuple-element.268, s32[]{:T(128)} %get-tuple-element.257, bf16[30,2048]{1,0:T(8,128)(2,1)S(1)} %dynamic-slice_bitcast_fusion.8), kind=kOutput, calls=%fused_computation.28.clone.1 | convolution fusion | flops 136311808 | bytes 208900 | tf_op jit(solution)/shard_map/while/body/eval_jaxpr/dot_general | solution.py:47
  91.8 1.4 %convert_reduce_fusion.26 = (f32[2048]{0:T(1024)S(1)}, f32[1024]{0:T(1024)S(1)}) fusion(bf16[3,30,2048]{2,1,0:T(8,128)(2,1)S(1)} %get-tuple-element.268, s32[]{:T(128)} %get-tuple-element.257, bf16[30,2048]{1,0:T(8,128)(2,1)S(1)} %dynamic-slice_bitcast_fusion.8), kind=kOutput, calls=%fused_computation.26.clone.1 | convolution fusion | flops 136311808 | bytes 208900 | tf_op jit(solution)/shard_map/while/body/eval_jaxpr/dot_general | solution.py:47
  96.6 1.4 %convert_reduce_fusion.27 = (f32[2048]{0:T(1024)S(1)}, f32[1024]{0:T(1024)S(1)}) fusion(bf16[3,30,2048]{2,1,0:T(8,128)(2,1)S(1)} %get-tuple-element.268, s32[]{:T(128)} %get-tuple-element.257, bf16[30,2048]{1,0:T(8,128)(2,1)S(1)} %dynamic-slice_bitcast_fusion.8), kind=kOutput, calls=%fused_computation.28.clone.1 | convolution fusion | flops 136311808 | bytes 208900 | tf_op jit(solution)/shard_map/while/body/eval_jaxpr/dot_general | solution.py:47
  99.7 1.6 %collective-permute-start.3 = (bf16[3,4096]{1,0:T(4,128)(2,1)S(1)}, bf16[3,4096]{1,0:T(4,128)(2,1)S(1)}, u32[]{:S(2)}, u32[]{:S(2)}) collective-permute-start(bf16[3,4096]{1,0:T(4,128)(2,1)S(1)} %convert_element_type.58), channel_id=1, source_target_pairs={{0,1},{1,0},{2,3},{3,2},{4,5},{5,4},{6,7},{7,6},{8,9},{9,8},{10,11... | collective-permute-start | bytes 73736 | tf_op jit(solution)/shard_map/ppermute | solution.py:31
  101.3 30.5 %while.34 = (s32[]{:T(128)}, f32[3,4096]{1,0:T(4,128)S(1)}, bf16[3,30,4096]{2,1,0:T(8,128)(2,1)S(1)}, s32[]{:T(128)}, s32[]{:T(128)}) while((s32[]{:T(128)}, f32[3,4096]{1,0:T(4,128)S(1)}, bf16[3,30,4096]{2,1,0:T(8,128)(2,1)S(1)}, s32[]{:T(128)}, s32[]{:T(128)}) %tuple.68), condition=%wide.region_12.13_spmd, body=%wide.region_7.12_spmd.sunk | while | flops 1073750016 | bytes 1884229 | solution.py:68
  101.5 2.4 %convert_reduce_fusion.20 = f32[1024]{0:T(1024)S(1)} fusion(bf16[30,4096]{1,0:T(8,128)(2,1)S(1)} %dynamic-slice_bitcast_fusion.6), kind=kOutput, calls=%fused_computation.clone.1 | convolution fusion | flops 268434432 | bytes 331776 | tf_op jit(solution)/shard_map/while/body/eval_jaxpr/dot_general | solution.py:47
  104.0 2.5 %convert_reduce_fusion.21 = f32[1024]{0:T(1024)S(1)} fusion(bf16[30,4096]{1,0:T(8,128)(2,1)S(1)} %dynamic-slice_bitcast_fusion.6), kind=kOutput, calls=%fused_computation.1.clone.1 | convolution fusion | flops 268434432 | bytes 331776 | tf_op jit(solution)/shard_map/while/body/eval_jaxpr/dot_general | solution.py:47
  106.4 2.5 %convert_reduce_fusion.22 = f32[1024]{0:T(1024)S(1)} fusion(bf16[30,4096]{1,0:T(8,128)(2,1)S(1)} %dynamic-slice_bitcast_fusion.6), kind=kOutput, calls=%fused_computation.2.clone.1 | convolution fusion | flops 268434432 | bytes 331776 | tf_op jit(solution)/shard_map/while/body/eval_jaxpr/dot_general | solution.py:47
  108.9 2.5 %convert_reduce_fusion.23 = f32[1024]{0:T(1024)S(1)} fusion(bf16[30,4096]{1,0:T(8,128)(2,1)S(1)} %dynamic-slice_bitcast_fusion.6), kind=kOutput, calls=%fused_computation.3.clone.1 | convolution fusion | flops 268434432 | bytes 331776 | tf_op jit(solution)/shard_map/while/body/eval_jaxpr/dot_general | solution.py:47
  111.6 2.4 %convert_reduce_fusion.20 = f32[1024]{0:T(1024)S(1)} fusion(bf16[30,4096]{1,0:T(8,128)(2,1)S(1)} %dynamic-slice_bitcast_fusion.6), kind=kOutput, calls=%fused_computation.clone.1 | convolution fusion | flops 268434432 | bytes 331776 | tf_op jit(solution)/shard_map/while/body/eval_jaxpr/dot_general | solution.py:47
  114.1 2.5 %convert_reduce_fusion.21 = f32[1024]{0:T(1024)S(1)} fusion(bf16[30,4096]{1,0:T(8,128)(2,1)S(1)} %dynamic-slice_bitcast_fusion.6), kind=kOutput, calls=%fused_computation.1.clone.1 | convolution fusion | flops 268434432 | bytes 331776 | tf_op jit(solution)/shard_map/while/body/eval_jaxpr/dot_general | solution.py:47
  116.5 2.5 %convert_reduce_fusion.22 = f32[1024]{0:T(1024)S(1)} fusion(bf16[30,4096]{1,0:T(8,128)(2,1)S(1)} %dynamic-slice_bitcast_fusion.6), kind=kOutput, calls=%fused_computation.2.clone.1 | convolution fusion | flops 268434432 | bytes 331776 | tf_op jit(solution)/shard_map/while/body/eval_jaxpr/dot_general | solution.py:47
  119.0 2.5 %convert_reduce_fusion.23 = f32[1024]{0:T(1024)S(1)} fusion(bf16[30,4096]{1,0:T(8,128)(2,1)S(1)} %dynamic-slice_bitcast_fusion.6), kind=kOutput, calls=%fused_computation.3.clone.1 | convolution fusion | flops 268434432 | bytes 331776 | tf_op jit(solution)/shard_map/while/body/eval_jaxpr/dot_general | solution.py:47
  121.7 2.4 %convert_reduce_fusion.20 = f32[1024]{0:T(1024)S(1)} fusion(bf16[30,4096]{1,0:T(8,128)(2,1)S(1)} %dynamic-slice_bitcast_fusion.6), kind=kOutput, calls=%fused_computation.clone.1 | convolution fusion | flops 268434432 | bytes 331776 | tf_op jit(solution)/shard_map/while/body/eval_jaxpr/dot_general | solution.py:47
  124.2 2.5 %convert_reduce_fusion.21 = f32[1024]{0:T(1024)S(1)} fusion(bf16[30,4096]{1,0:T(8,128)(2,1)S(1)} %dynamic-slice_bitcast_fusion.6), kind=kOutput, calls=%fused_computation.1.clone.1 | convolution fusion | flops 268434432 | bytes 331776 | tf_op jit(solution)/shard_map/while/body/eval_jaxpr/dot_general | solution.py:47
  126.6 2.5 %convert_reduce_fusion.22 = f32[1024]{0:T(1024)S(1)} fusion(bf16[30,4096]{1,0:T(8,128)(2,1)S(1)} %dynamic-slice_bitcast_fusion.6), kind=kOutput, calls=%fused_computation.2.clone.1 | convolution fusion | flops 268434432 | bytes 331776 | tf_op jit(solution)/shard_map/while/body/eval_jaxpr/dot_general | solution.py:47
  129.1 2.5 %convert_reduce_fusion.23 = f32[1024]{0:T(1024)S(1)} fusion(bf16[30,4096]{1,0:T(8,128)(2,1)S(1)} %dynamic-slice_bitcast_fusion.6), kind=kOutput, calls=%fused_computation.3.clone.1 | convolution fusion | flops 268434432 | bytes 331776 | tf_op jit(solution)/shard_map/while/body/eval_jaxpr/dot_general | solution.py:47
  (96 shorter events, 23.3 us)
Async XLA Ops:
  0.0 23.0 %copy-start.1 = (f32[1,1,6400]{2,1,0:T(1,128)S(1)}, f32[1,1,6400]{2,1,0:T(1,128)}, u32[]{:S(2)}) copy-start(f32[1,1,6400]{2,1,0:T(1,128)} %param.9) | copy-start | bytes 76804
  0.0 17.3 %all-to-all-start = ((f32[16,1,3840]{2,1,0:T(1,128)}), f32[16,1,3840]{2,1,0:T(1,128)S(1)}, u32[]{:S(2)}, u32[]{:S(2)}) async-start(f32[16,1,3840]{2,1,0:T(1,128)} %bitcast.93), calls=%async_computation | async-start | bytes 491520 | tf_op jit(solution)/shard_map/all_to_all | solution.py:96
  18.3 28.7 %collective-permute-start.1 = (f32[15,4096]{1,0:T(8,128)S(1)}, f32[15,4096]{1,0:T(8,128)S(1)}, u32[]{:S(2)}, u32[]{:S(2)}) collective-permute-start(f32[15,4096]{1,0:T(8,128)S(1)} %bitcast.86), channel_id=1, source_target_pairs={{0,2},{2,4},{4,6},{6,8},{8,10},{10,12},{12,14},{14,16},{16,18},{18... | collective-permute-start | bytes 737288 | tf_op jit(solution)/shard_map/ppermute | solution.py:21
  20.4 26.6 %collective-permute-start = (f32[10,4096]{1,0:T(8,128)S(1)}, f32[10,4096]{1,0:T(8,128)S(1)}, u32[]{:S(2)}, u32[]{:S(2)}) collective-permute-start(f32[10,4096]{1,0:T(8,128)S(1)} %bitcast.92), channel_id=1, source_target_pairs={{0,4},{2,6},{4,8},{6,10},{8,12},{10,14},{12,16},{14,18},{16,20},{1... | collective-permute-start | bytes 491528 | tf_op jit(solution)/shard_map/ppermute | solution.py:21
  57.3 1.6 %copy-start = (f32[3,4096]{1,0:T(4,128)S(1)}, f32[3,4096]{1,0:T(4,128)}, u32[]{:S(2)}) copy-start(f32[3,4096]{1,0:T(4,128)} %get-tuple-element.128) | copy-start | bytes 147460
  61.3 19.9 %collective-permute-start.2 = (bf16[3,30,4096]{2,1,0:T(8,128)(2,1)S(1)}, bf16[3,30,4096]{2,1,0:T(8,128)(2,1)S(1)}, u32[]{:S(2)}, u32[]{:S(2)}) collective-permute-start(bf16[3,30,4096]{2,1,0:T(8,128)(2,1)S(1)} %multiply_convert_fusion), channel_id=1, source_target_pairs={{0,1},{1,0},{2,3},{3,2},{4,5},{5,4},{6,7},{7,6},{8,9},{9,8},{10,11... | collective-permute-start | bytes 2211848 | tf_op jit(solution)/shard_map/ppermute | solution.py:31
  99.7 32.1 %collective-permute-start.3 = (bf16[3,4096]{1,0:T(4,128)(2,1)S(1)}, bf16[3,4096]{1,0:T(4,128)(2,1)S(1)}, u32[]{:S(2)}, u32[]{:S(2)}) collective-permute-start(bf16[3,4096]{1,0:T(4,128)(2,1)S(1)} %convert_element_type.58), channel_id=1, source_target_pairs={{0,1},{1,0},{2,3},{3,2},{4,5},{5,4},{6,7},{7,6},{8,9},{9,8},{10,11... | collective-permute-start | bytes 73736 | tf_op jit(solution)/shard_map/ppermute | solution.py:31
where the time goes:
time: 133 us; the launch traced here: 132 us
  matrix products  45.7 us (34%)
  waiting for transfers between devices  28 us (21%)
  blocking collectives  22.3 us (17%)
  starting transfers between devices  15 us (11%)
  local copies, waits for them, and re-layouts  12.9 us (10%)
  other arithmetic  7.66 us (6%)
    dot_general x24, matrix products, block_magnitude(): lax.dot_general(left_part[:, offset:offset + block_rows], right_part, (((...  45.7 us
    all_gather x1, blocking collectives, time_block_rows(): prior_all = lax.all_gather(prior_bars, 'tm', axis=1, tiled=True)  22.3 us
    ppermute x2, waiting for transfers between devices, swapped(): return lax.ppermute(block, axis, route)  18.2 us
    all_to_all x1, waiting for transfers between devices, time_block_rows(): lax.all_to_all(outgoing, 'tm', split_axis=0, concat_axis=1, tiled=True)  9.75 us
    all_to_all x1, starting transfers between devices, time_block_rows(): lax.all_to_all(outgoing, 'tm', split_axis=0, concat_axis=1, tiled=True)  7.55 us
    another operation x7, local copies, waits for them, and re-layouts, window_stack(): jnp.stack([groups[offset:offset + WIN_DEV] for offset in range(SPAN // ST...  7.1 us
    ppermute x2, starting transfers between devices, from_behind(): return lax.ppermute(x, axis, pairs)  4.3 us
    reduce_sum x6, other arithmetic, window_stack(): centred = values - jnp.mean(values, axis=1, keepdims=True)  3.52 us
  transfers between devices with their start and end apart: 5, of which 2 were waited for; matrix products, arithmetic and copies ran while one was open for 24% of the time, Pallas kernels for 0%

commit v1 on v0

--- a/solution.py
+++ b/solution.py
@@ -15,12 +15,6 @@
 FLOOR_SQUARES = 1.0
 
 
-def from_behind(x, axis, by):
-    size = lax.axis_size(axis)
-    pairs = [(i, i + by) for i in range(size) if 0 <= i + by < size]
-    return lax.ppermute(x, axis, pairs)
-
-
 def swapped(block, axis, distance):
     count = lax.axis_size(axis)
     route = []
@@ -33,11 +27,12 @@
 
 def window_stack(extended):
     columns = extended.shape[1]
+    count = (extended.shape[0] - SPAN) // STRIDE + 1
     groups = extended.reshape(-1, STRIDE, columns)
     stacked = jnp.stack(
-        [groups[offset : offset + WIN_DEV] for offset in range(SPAN // STRIDE)], axis=1
+        [groups[offset : offset + count] for offset in range(SPAN // STRIDE)], axis=1
     )
-    values = stacked.reshape(WIN_DEV, SPAN, columns)
+    values = stacked.reshape(count, SPAN, columns)
     centred = values - jnp.mean(values, axis=1, keepdims=True)
     squares = jnp.sum(centred * centred, axis=1, keepdims=True)
     return (centred * lax.rsqrt(jnp.maximum(squares, FLOOR_SQUARES))).astype(jnp.bfloat16)
@@ -85,41 +80,21 @@
     return lax.map(both_one_window, (own_windows, other_windows))
 
 
-def earlier_rows(tail_rows, distance):
-    return from_behind(tail_rows, "tm", distance)
-
-
-def time_block_rows(tick_bars, prior_bars):
+def local_windows(tick_bars, prior_bars):
     groups = lax.axis_size("tm")
     group_cols = ASSETS // (2 * groups)
-    outgoing = tick_bars.reshape(groups, 1, -1)
-    arrived = lax.all_to_all(outgoing, "tm", split_axis=0, concat_axis=1, tiled=True)
-    block_len = arrived.shape[2] // group_cols
-    own_rows = jnp.transpose(arrived.reshape(groups, block_len, group_cols), (1, 0, 2)).reshape(
-        block_len, groups * group_cols
+    series = jnp.concatenate(
+        [prior_bars.reshape(-1, group_cols), tick_bars.reshape(-1, group_cols)], axis=0
     )
-    prior_all = lax.all_gather(prior_bars, "tm", axis=1, tiled=True)
-    series_prior = jnp.transpose(prior_all.reshape(groups, LEAD, group_cols), (1, 0, 2)).reshape(
-        LEAD, groups * group_cols
-    )
-    reach = (LEAD + block_len - 1) // block_len
-    earlier = []
-    for distance in range(reach, 0, -1):
-        needed = min(block_len, LEAD - (distance - 1) * block_len)
-        earlier.append(earlier_rows(own_rows[block_len - needed :], distance))
-    history = jnp.concatenate(earlier, axis=0)
-    position = lax.axis_index("tm")
-    first_row = position * block_len
-    padded = jnp.concatenate([series_prior, jnp.zeros_like(series_prior)], axis=0)
-    from_prior = lax.dynamic_slice_in_dim(padded, jnp.minimum(first_row, LEAD), LEAD, 0)
-    before_start = first_row - LEAD + jnp.arange(LEAD, dtype=jnp.int32) < 0
-    history = jnp.where(before_start[:, None], from_prior, history)
-    return jnp.concatenate([history, own_rows], axis=0)
+    return window_stack(series)
 
 
 def shards(tick_bars, prior_bars):
-    extended = time_block_rows(tick_bars, prior_bars)
-    scaled = window_stack(extended)
+    groups = lax.axis_size("tm")
+    outgoing = local_windows(tick_bars, prior_bars)
+    arrived = lax.all_to_all(outgoing, "tm", split_axis=0, concat_axis=0, tiled=True)
+    arrived = arrived.reshape(groups, WIN_DEV, SPAN, -1)
+    scaled = jnp.transpose(arrived, (1, 2, 0, 3)).reshape(WIN_DEV, SPAN, -1)
     columns = scaled.shape[2]
     empty = jnp.zeros((WIN_DEV, columns), jnp.float32)
     partner = swapped(scaled, "asset", 0)

time: 133 us -> 113 us (0.85)
  starting transfers between devices: 15 us -> 3.12 us
  waiting for transfers between devices: 28 us -> 18.8 us
  blocking collectives: 22.3 us -> 27.3 us
  local copies, waits for them, and re-layouts: 12.9 us -> 8.66 us
    all_to_all x0 -> x1, blocking collectives: none -> 27.3 us  [shards(): lax.all_to_all(outgoing, 'tm', split_axis=0, concat_axis=0, tiled=True)]
    all_gather x1 -> x0, blocking collectives: 22.3 us -> none  [time_block_rows(): prior_all = lax.all_gather(prior_bars, 'tm', axis=1, tiled=True)]
    all_to_all x1 -> x0, waiting for transfers between devices: 9.75 us -> none  [time_block_rows(): lax.all_to_all(outgoing, 'tm', split_axis=0, concat_axis=1, tiled=True)]
    all_to_all x1 -> x0, starting transfers between devices: 7.55 us -> none  [time_block_rows(): lax.all_to_all(outgoing, 'tm', split_axis=0, concat_axis=1, tiled=True)]
    ppermute x2 -> x0, starting transfers between devices: 4.3 us -> none  [from_behind(): return lax.ppermute(x, axis, pairs)]
    another operation x13, local copies, waits for them, and re-layouts: 7.14 us -> 4.15 us  [the longest x7 4.1 us: window_stack(): jnp.stack([groups[offset:offset + count] for offset in range(SPAN // STRI...]
    unnamed x0 -> x2, other arithmetic: none -> 2.98 us
    reshape x3, local copies, waits for them, and re-layouts: 1.88 us -> 0.52 us  [the longest x1 0.44 us: shards(): scaled = jnp.transpose(arrived, (1, 2, 0, 3)).reshape(WIN_DEV, SPAN, -1)]
  transfers between devices with their start and end apart: 5 -> 2, of which waited for: 2 -> 1; matrix products, arithmetic and copies ran while one was open for 24% -> 27% of each run, Pallas kernels for 0% -> 0%
where the time goes in v1:
time: 113 us
  matrix products  45.7 us (40%)
  blocking collectives  27.3 us (24%)
  waiting for transfers between devices  18.8 us (17%)
  local copies, waits for them, and re-layouts  8.66 us (8%)
  other arithmetic  8.58 us (8%)
  starting transfers between devices  3.12 us (3%)
    dot_general x24, matrix products, block_magnitude(): lax.dot_general(left_part[:, offset:offset + block_rows], right_part, (((...  45.7 us
    all_to_all x1, blocking collectives, shards(): lax.all_to_all(outgoing, 'tm', split_axis=0, concat_axis=0, tiled=True)  27.3 us
    ppermute x2, waiting for transfers between devices, swapped(): return lax.ppermute(block, axis, route)  18.8 us
    another operation x7, local copies, waits for them, and re-layouts, window_stack(): jnp.stack([groups[offset:offset + count] for offset in range(SPAN // STRI...  4.1 us
    reduce_sum x6, other arithmetic, window_stack(): centred = values - jnp.mean(values, axis=1, keepdims=True)  3.44 us
    ppermute x2, starting transfers between devices, swapped(): return lax.ppermute(block, axis, route)  3.12 us
    unnamed x2, other arithmetic  2.98 us
  transfers between devices with their start and end apart: 2, of which 1 were waited for; matrix products, arithmetic and copies ran while one was open for 27% of the time, Pallas kernels for 0%

profile of v1, /device:TPU:0, one launch (start us, length us, event | category | flops | bytes accessed | tf_op | source)
XLA Modules:
  0.0 113.0 jit_solution(9174448222791185204)
XLA Ops:
  0.5 2.2 %reduce.14 = f32[61440]{0:T(1024)S(1)} reduce(f32[1,1,61440]{2,1,0:T(1,128)} %param.8, f32[]{:T(128)} %broadcast.28), dimensions={0,1}, to_apply=%param.8.reduce_sub_computation.5 | reduce | bytes 491524 | tf_op args[0]
  13.1 27.3 %all_to_all.5 = bf16[48,30,256]{2,1,0:T(8,128)(2,1)S(1)} all-to-all(bf16[48,30,256]{2,1,0:T(8,128)(2,1)S(1)} %copy.9), channel_id=1, replica_groups=mesh['tm'=16,'asset'=2] {'tm'}, dimensions={0} | all-to-all | bytes 1474560 | tf_op jit(solution)/shard_map/all_to_all | solution.py:95
  41.3 1.6 %collective-permute-start = (bf16[3,30,4096]{2,1,0:T(8,128)(2,1)S(1)}, bf16[3,30,4096]{2,1,0:T(8,128)(2,1)S(1)}, u32[]{:S(2)}, u32[]{:S(2)}) collective-permute-start(bf16[3,30,4096]{2,1,0:T(8,128)(2,1)S(1)} %reshape.72), channel_id=1, source_target_pairs={{0,1},{1,0},{2,3},{3,2},{4,5},{5,4},{6,7},{7,6},{8,9},{9,8},{10,11... | collective-permute-start | bytes 2211848 | tf_op jit(solution)/shard_map/ppermute | solution.py:25
  42.9 18.8 %collective-permute-done = bf16[3,30,4096]{2,1,0:T(8,128)(2,1)S(1)} collective-permute-done((bf16[3,30,4096]{2,1,0:T(8,128)(2,1)S(1)}, bf16[3,30,4096]{2,1,0:T(8,128)(2,1)S(1)}, u32[]{:S(2)}, u32[]{:S(2)}) %collective-permute-start) | collective-permute-done | bytes 737312 | tf_op jit(solution)/shard_map/ppermute | solution.py:25
  61.8 9.1 %while.35 = (s32[]{:T(128)}, f32[3,2048]{1,0:T(4,128)S(1)}, f32[3,2048]{1,0:T(4,128)S(1)}, bf16[3,30,2048]{2,1,0:T(8,128)(2,1)S(1)}, bf16[3,30,2048]{2,1,0:T(8,128)(2,1)S(1)}, /*index=5*/s32[]{:T(128)}, s32[]{:T(128)}) while((s32[]{:T(128)}, f32[3,2048]{1,0:T(4,128)S(1)}, f32[3,2048]{1,0:T(4,128)S(1)}, bf16[3,30,2048]{2,1,0:T(8,128)(2,1)S(1)}, ...), condition=%wide.region_18.19_spmd, body=%wide.region_13.18_spmd.sunk | while | flops 272627712 | bytes 737377 | solution.py:80
  61.8 1.4 %convert_reduce_fusion.25 = (f32[2048]{0:T(1024)S(1)}, f32[1024]{0:T(1024)S(1)}) fusion(bf16[3,30,2048]{2,1,0:T(8,128)(2,1)S(1)} %get-tuple-element.289, s32[]{:T(128)} %get-tuple-element.278, bf16[30,2048]{1,0:T(8,128)(2,1)S(1)} %dynamic-slice_bitcast_fusion.7), kind=kOutput, calls=%fused_computation.12.clone.1 | convolution fusion | flops 136311808 | bytes 208900 | tf_op jit(solution)/shard_map/while/body/eval_jaxpr/dot_general | solution.py:42
  63.2 1.4 %convert_reduce_fusion.24 = (f32[2048]{0:T(1024)S(1)}, f32[1024]{0:T(1024)S(1)}) fusion(bf16[3,30,2048]{2,1,0:T(8,128)(2,1)S(1)} %get-tuple-element.289, s32[]{:T(128)} %get-tuple-element.278, bf16[30,2048]{1,0:T(8,128)(2,1)S(1)} %dynamic-slice_bitcast_fusion.7), kind=kOutput, calls=%fused_computation.10.clone.1 | convolution fusion | flops 136311808 | bytes 208900 | tf_op jit(solution)/shard_map/while/body/eval_jaxpr/dot_general | solution.py:42
  64.9 1.4 %convert_reduce_fusion.25 = (f32[2048]{0:T(1024)S(1)}, f32[1024]{0:T(1024)S(1)}) fusion(bf16[3,30,2048]{2,1,0:T(8,128)(2,1)S(1)} %get-tuple-element.289, s32[]{:T(128)} %get-tuple-element.278, bf16[30,2048]{1,0:T(8,128)(2,1)S(1)} %dynamic-slice_bitcast_fusion.7), kind=kOutput, calls=%fused_computation.12.clone.1 | convolution fusion | flops 136311808 | bytes 208900 | tf_op jit(solution)/shard_map/while/body/eval_jaxpr/dot_general | solution.py:42
  66.2 1.4 %convert_reduce_fusion.24 = (f32[2048]{0:T(1024)S(1)}, f32[1024]{0:T(1024)S(1)}) fusion(bf16[3,30,2048]{2,1,0:T(8,128)(2,1)S(1)} %get-tuple-element.289, s32[]{:T(128)} %get-tuple-element.278, bf16[30,2048]{1,0:T(8,128)(2,1)S(1)} %dynamic-slice_bitcast_fusion.7), kind=kOutput, calls=%fused_computation.10.clone.1 | convolution fusion | flops 136311808 | bytes 208900 | tf_op jit(solution)/shard_map/while/body/eval_jaxpr/dot_general | solution.py:42
  67.9 1.4 %convert_reduce_fusion.25 = (f32[2048]{0:T(1024)S(1)}, f32[1024]{0:T(1024)S(1)}) fusion(bf16[3,30,2048]{2,1,0:T(8,128)(2,1)S(1)} %get-tuple-element.289, s32[]{:T(128)} %get-tuple-element.278, bf16[30,2048]{1,0:T(8,128)(2,1)S(1)} %dynamic-slice_bitcast_fusion.7), kind=kOutput, calls=%fused_computation.12.clone.1 | convolution fusion | flops 136311808 | bytes 208900 | tf_op jit(solution)/shard_map/while/body/eval_jaxpr/dot_general | solution.py:42
  69.3 1.4 %convert_reduce_fusion.24 = (f32[2048]{0:T(1024)S(1)}, f32[1024]{0:T(1024)S(1)}) fusion(bf16[3,30,2048]{2,1,0:T(8,128)(2,1)S(1)} %get-tuple-element.289, s32[]{:T(128)} %get-tuple-element.278, bf16[30,2048]{1,0:T(8,128)(2,1)S(1)} %dynamic-slice_bitcast_fusion.7), kind=kOutput, calls=%fused_computation.10.clone.1 | convolution fusion | flops 136311808 | bytes 208900 | tf_op jit(solution)/shard_map/while/body/eval_jaxpr/dot_general | solution.py:42
  71.0 9.1 %while.36 = (s32[]{:T(128)}, f32[3,2048]{1,0:T(4,128)S(1)}, f32[3,2048]{1,0:T(4,128)S(1)}, bf16[3,30,2048]{2,1,0:T(8,128)(2,1)S(1)}, bf16[3,30,2048]{2,1,0:T(8,128)(2,1)S(1)}, /*index=5*/s32[]{:T(128)}, s32[]{:T(128)}) while((s32[]{:T(128)}, f32[3,2048]{1,0:T(4,128)S(1)}, f32[3,2048]{1,0:T(4,128)S(1)}, bf16[3,30,2048]{2,1,0:T(8,128)(2,1)S(1)}, ...), condition=%wide.region_24.25_spmd, body=%wide.region_19.24_spmd.sunk | while | flops 272627712 | bytes 737377 | solution.py:80
  71.0 1.4 %convert_reduce_fusion.27 = (f32[2048]{0:T(1024)S(1)}, f32[1024]{0:T(1024)S(1)}) fusion(bf16[3,30,2048]{2,1,0:T(8,128)(2,1)S(1)} %get-tuple-element.268, s32[]{:T(128)} %get-tuple-element.257, bf16[30,2048]{1,0:T(8,128)(2,1)S(1)} %dynamic-slice_bitcast_fusion.8), kind=kOutput, calls=%fused_computation.28.clone.1 | convolution fusion | flops 136311808 | bytes 208900 | tf_op jit(solution)/shard_map/while/body/eval_jaxpr/dot_general | solution.py:42
  72.4 1.4 %convert_reduce_fusion.26 = (f32[2048]{0:T(1024)S(1)}, f32[1024]{0:T(1024)S(1)}) fusion(bf16[3,30,2048]{2,1,0:T(8,128)(2,1)S(1)} %get-tuple-element.268, s32[]{:T(128)} %get-tuple-element.257, bf16[30,2048]{1,0:T(8,128)(2,1)S(1)} %dynamic-slice_bitcast_fusion.8), kind=kOutput, calls=%fused_computation.26.clone.1 | convolution fusion | flops 136311808 | bytes 208900 | tf_op jit(solution)/shard_map/while/body/eval_jaxpr/dot_general | solution.py:42
  74.1 1.4 %convert_reduce_fusion.27 = (f32[2048]{0:T(1024)S(1)}, f32[1024]{0:T(1024)S(1)}) fusion(bf16[3,30,2048]{2,1,0:T(8,128)(2,1)S(1)} %get-tuple-element.268, s32[]{:T(128)} %get-tuple-element.257, bf16[30,2048]{1,0:T(8,128)(2,1)S(1)} %dynamic-slice_bitcast_fusion.8), kind=kOutput, calls=%fused_computation.28.clone.1 | convolution fusion | flops 136311808 | bytes 208900 | tf_op jit(solution)/shard_map/while/body/eval_jaxpr/dot_general | solution.py:42
  75.4 1.4 %convert_reduce_fusion.26 = (f32[2048]{0:T(1024)S(1)}, f32[1024]{0:T(1024)S(1)}) fusion(bf16[3,30,2048]{2,1,0:T(8,128)(2,1)S(1)} %get-tuple-element.268, s32[]{:T(128)} %get-tuple-element.257, bf16[30,2048]{1,0:T(8,128)(2,1)S(1)} %dynamic-slice_bitcast_fusion.8), kind=kOutput, calls=%fused_computation.26.clone.1 | convolution fusion | flops 136311808 | bytes 208900 | tf_op jit(solution)/shard_map/while/body/eval_jaxpr/dot_general | solution.py:42
  77.1 1.4 %convert_reduce_fusion.27 = (f32[2048]{0:T(1024)S(1)}, f32[1024]{0:T(1024)S(1)}) fusion(bf16[3,30,2048]{2,1,0:T(8,128)(2,1)S(1)} %get-tuple-element.268, s32[]{:T(128)} %get-tuple-element.257, bf16[30,2048]{1,0:T(8,128)(2,1)S(1)} %dynamic-slice_bitcast_fusion.8), kind=kOutput, calls=%fused_computation.28.clone.1 | convolution fusion | flops 136311808 | bytes 208900 | tf_op jit(solution)/shard_map/while/body/eval_jaxpr/dot_general | solution.py:42
  78.5 1.4 %convert_reduce_fusion.26 = (f32[2048]{0:T(1024)S(1)}, f32[1024]{0:T(1024)S(1)}) fusion(bf16[3,30,2048]{2,1,0:T(8,128)(2,1)S(1)} %get-tuple-element.268, s32[]{:T(128)} %get-tuple-element.257, bf16[30,2048]{1,0:T(8,128)(2,1)S(1)} %dynamic-slice_bitcast_fusion.8), kind=kOutput, calls=%fused_computation.26.clone.1 | convolution fusion | flops 136311808 | bytes 208900 | tf_op jit(solution)/shard_map/while/body/eval_jaxpr/dot_general | solution.py:42
  80.2 1.6 %collective-permute-start.1 = (bf16[3,4096]{1,0:T(4,128)(2,1)S(1)}, bf16[3,4096]{1,0:T(4,128)(2,1)S(1)}, u32[]{:S(2)}, u32[]{:S(2)}) collective-permute-start(bf16[3,4096]{1,0:T(4,128)(2,1)S(1)} %convert_element_type.58), channel_id=1, source_target_pairs={{0,1},{1,0},{2,3},{3,2},{4,5},{5,4},{6,7},{7,6},{8,9},{9,8},{10,11... | collective-permute-start | bytes 73736 | tf_op jit(solution)/shard_map/ppermute | solution.py:25
  81.8 30.5 %while.34 = (s32[]{:T(128)}, f32[3,4096]{1,0:T(4,128)S(1)}, bf16[3,30,4096]{2,1,0:T(8,128)(2,1)S(1)}, s32[]{:T(128)}, s32[]{:T(128)}) while((s32[]{:T(128)}, f32[3,4096]{1,0:T(4,128)S(1)}, bf16[3,30,4096]{2,1,0:T(8,128)(2,1)S(1)}, s32[]{:T(128)}, s32[]{:T(128)}) %tuple.68), condition=%wide.region_12.13_spmd, body=%wide.region_7.12_spmd.sunk | while | flops 1073750016 | bytes 1884229 | solution.py:63
  82.0 2.4 %convert_reduce_fusion.20 = f32[1024]{0:T(1024)S(1)} fusion(bf16[30,4096]{1,0:T(8,128)(2,1)S(1)} %dynamic-slice_bitcast_fusion.6), kind=kOutput, calls=%fused_computation.clone.1 | convolution fusion | flops 268434432 | bytes 331776 | tf_op jit(solution)/shard_map/while/body/eval_jaxpr/dot_general | solution.py:42
  84.5 2.5 %convert_reduce_fusion.21 = f32[1024]{0:T(1024)S(1)} fusion(bf16[30,4096]{1,0:T(8,128)(2,1)S(1)} %dynamic-slice_bitcast_fusion.6), kind=kOutput, calls=%fused_computation.1.clone.1 | convolution fusion | flops 268434432 | bytes 331776 | tf_op jit(solution)/shard_map/while/body/eval_jaxpr/dot_general | solution.py:42
  86.9 2.5 %convert_reduce_fusion.22 = f32[1024]{0:T(1024)S(1)} fusion(bf16[30,4096]{1,0:T(8,128)(2,1)S(1)} %dynamic-slice_bitcast_fusion.6), kind=kOutput, calls=%fused_computation.2.clone.1 | convolution fusion | flops 268434432 | bytes 331776 | tf_op jit(solution)/shard_map/while/body/eval_jaxpr/dot_general | solution.py:42
  89.4 2.5 %convert_reduce_fusion.23 = f32[1024]{0:T(1024)S(1)} fusion(bf16[30,4096]{1,0:T(8,128)(2,1)S(1)} %dynamic-slice_bitcast_fusion.6), kind=kOutput, calls=%fused_computation.3.clone.1 | convolution fusion | flops 268434432 | bytes 331776 | tf_op jit(solution)/shard_map/while/body/eval_jaxpr/dot_general | solution.py:42
  92.1 2.4 %convert_reduce_fusion.20 = f32[1024]{0:T(1024)S(1)} fusion(bf16[30,4096]{1,0:T(8,128)(2,1)S(1)} %dynamic-slice_bitcast_fusion.6), kind=kOutput, calls=%fused_computation.clone.1 | convolution fusion | flops 268434432 | bytes 331776 | tf_op jit(solution)/shard_map/while/body/eval_jaxpr/dot_general | solution.py:42
  94.6 2.5 %convert_reduce_fusion.21 = f32[1024]{0:T(1024)S(1)} fusion(bf16[30,4096]{1,0:T(8,128)(2,1)S(1)} %dynamic-slice_bitcast_fusion.6), kind=kOutput, calls=%fused_computation.1.clone.1 | convolution fusion | flops 268434432 | bytes 331776 | tf_op jit(solution)/shard_map/while/body/eval_jaxpr/dot_general | solution.py:42
  97.0 2.5 %convert_reduce_fusion.22 = f32[1024]{0:T(1024)S(1)} fusion(bf16[30,4096]{1,0:T(8,128)(2,1)S(1)} %dynamic-slice_bitcast_fusion.6), kind=kOutput, calls=%fused_computation.2.clone.1 | convolution fusion | flops 268434432 | bytes 331776 | tf_op jit(solution)/shard_map/while/body/eval_jaxpr/dot_general | solution.py:42
  99.5 2.5 %convert_reduce_fusion.23 = f32[1024]{0:T(1024)S(1)} fusion(bf16[30,4096]{1,0:T(8,128)(2,1)S(1)} %dynamic-slice_bitcast_fusion.6), kind=kOutput, calls=%fused_computation.3.clone.1 | convolution fusion | flops 268434432 | bytes 331776 | tf_op jit(solution)/shard_map/while/body/eval_jaxpr/dot_general | solution.py:42
  102.3 2.4 %convert_reduce_fusion.20 = f32[1024]{0:T(1024)S(1)} fusion(bf16[30,4096]{1,0:T(8,128)(2,1)S(1)} %dynamic-slice_bitcast_fusion.6), kind=kOutput, calls=%fused_computation.clone.1 | convolution fusion | flops 268434432 | bytes 331776 | tf_op jit(solution)/shard_map/while/body/eval_jaxpr/dot_general | solution.py:42
  104.7 2.5 %convert_reduce_fusion.21 = f32[1024]{0:T(1024)S(1)} fusion(bf16[30,4096]{1,0:T(8,128)(2,1)S(1)} %dynamic-slice_bitcast_fusion.6), kind=kOutput, calls=%fused_computation.1.clone.1 | convolution fusion | flops 268434432 | bytes 331776 | tf_op jit(solution)/shard_map/while/body/eval_jaxpr/dot_general | solution.py:42
  107.2 2.5 %convert_reduce_fusion.22 = f32[1024]{0:T(1024)S(1)} fusion(bf16[30,4096]{1,0:T(8,128)(2,1)S(1)} %dynamic-slice_bitcast_fusion.6), kind=kOutput, calls=%fused_computation.2.clone.1 | convolution fusion | flops 268434432 | bytes 331776 | tf_op jit(solution)/shard_map/while/body/eval_jaxpr/dot_general | solution.py:42
  109.6 2.5 %convert_reduce_fusion.23 = f32[1024]{0:T(1024)S(1)} fusion(bf16[30,4096]{1,0:T(8,128)(2,1)S(1)} %dynamic-slice_bitcast_fusion.6), kind=kOutput, calls=%fused_computation.3.clone.1 | convolution fusion | flops 268434432 | bytes 331776 | tf_op jit(solution)/shard_map/while/body/eval_jaxpr/dot_general | solution.py:42
  (79 shorter events, 15.1 us)
Async XLA Ops:
  11.4 0.8 copy-start
  41.3 20.4 %collective-permute-start = (bf16[3,30,4096]{2,1,0:T(8,128)(2,1)S(1)}, bf16[3,30,4096]{2,1,0:T(8,128)(2,1)S(1)}, u32[]{:S(2)}, u32[]{:S(2)}) collective-permute-start(bf16[3,30,4096]{2,1,0:T(8,128)(2,1)S(1)} %reshape.72), channel_id=1, source_target_pairs={{0,1},{1,0},{2,3},{3,2},{4,5},{5,4},{6,7},{7,6},{8,9},{9,8},{10,11... | collective-permute-start | bytes 2211848 | tf_op jit(solution)/shard_map/ppermute | solution.py:25
  80.2 32.1 %collective-permute-start.1 = (bf16[3,4096]{1,0:T(4,128)(2,1)S(1)}, bf16[3,4096]{1,0:T(4,128)(2,1)S(1)}, u32[]{:S(2)}, u32[]{:S(2)}) collective-permute-start(bf16[3,4096]{1,0:T(4,128)(2,1)S(1)} %convert_element_type.58), channel_id=1, source_target_pairs={{0,1},{1,0},{2,3},{3,2},{4,5},{5,4},{6,7},{7,6},{8,9},{9,8},{10,11... | collective-permute-start | bytes 73736 | tf_op jit(solution)/shard_map/ppermute | solution.py:25

commit v2 on v1

v2 whole, which is shorter than its diff:
```python
import math

import jax
import jax.numpy as jnp
from jax import lax
from jax.experimental import pallas as pl
from jax.experimental.pallas import tpu as pltpu
from jax.sharding import PartitionSpec as P

ASSETS = 8192
SPAN = 30
STRIDE = 5
WIN_DEV = 3
LEAD = 25
DEPTH = 32
TILE = 256
LANES = 128
SUBLANES = 8


FLOOR_SQUARES = 1.0


def swapped(block, axis, distance):
    count = lax.axis_size(axis)
    route = []
    for low in range(count):
        high = low | 1 << distance
        if high != low and high < count:
            route += [(low, high), (high, low)]
    return lax.ppermute(block, axis, route)


def window_stack(extended):
    columns = extended.shape[1]
    count = (extended.shape[0] - SPAN) // STRIDE + 1
    groups = extended.reshape(-1, STRIDE, columns)
    stacked = jnp.stack(
        [groups[offset : offset + count] for offset in range(SPAN // STRIDE)], axis=1
    )
    values = stacked.reshape(count, SPAN, columns)
    centred = values - jnp.mean(values, axis=1, keepdims=True)
    squares = jnp.sum(centred * centred, axis=1, keepdims=True)
    scaled = (centred * lax.rsqrt(jnp.maximum(squares, FLOOR_SQUARES))).astype(jnp.bfloat16)
    return jnp.pad(scaled, ((0, 0), (0, DEPTH - SPAN), (0, 0)))


def strip_totals(rows_t, source, start, width, column_sums, own_first):
    rows = rows_t.shape[0]
    row_partial = jnp.zeros((rows, LANES), jnp.float32)
    for offset in range(0, width, TILE):
        at = pl.ds(pl.multiple_of(start + offset, TILE), TILE)
        magnitude = jnp.abs(jnp.dot(rows_t, source[:, at], preferred_element_type=jnp.float32))
        row_partial = row_partial + (magnitude[:, :LANES] + magnitude[:, LANES:])
        if offset or not own_first:
            folded = jnp.sum(magnitude.reshape(rows // SUBLANES, SUBLANES, TILE), axis=0)
            column_sums[:, at] = column_sums[:, at] + folded
    return row_partial


def row_vector(row_partial):
    return jnp.sum(row_partial.T, axis=0, keepdims=True)


def diagonal_kernel(own, out, wrapped, column_sums):
    columns = own.shape[2]
    half = columns // 2
    wrapped[:, :columns] = own[0]
    wrapped[:, columns:] = own[0, :, : wrapped.shape[1] - columns]
    column_sums[...] = jnp.zeros_like(column_sums)

    def step(index, carry):
        for upper in range(2):
            first = pl.multiple_of(index * TILE + upper * half, TILE)
            rows_t = wrapped[:, pl.ds(first, TILE)].T
            width = half if upper else half + TILE
            partial = strip_totals(rows_t, wrapped, first, width, column_sums, True)
            out[0, :, pl.ds(first, TILE)] = row_vector(partial)
        return carry

    lax.fori_loop(0, half // TILE, step, 0)
    folded = jnp.sum(column_sums[...], axis=0, keepdims=True)
    out[0] = out[0] + folded[:, :columns]
    spill = columns - half
    out[0, :, :spill] = out[0, :, :spill] + folded[:, columns : columns + spill]


def cross_kernel(tile, own, other, row_out, column_out, column_sums):
    columns = own.shape[2]
    half = columns // 2
    column_sums[...] = jnp.zeros_like(column_sums)

    def step(index, carry):
        for upper in range(2):
            first = pl.multiple_of(index * TILE + upper * half, TILE)
            rows_t = own[0, :, pl.ds(first, TILE)].T
            target = lax.rem(tile[0] + upper, 2) * half
            partial = strip_totals(rows_t, other.at[0], target, half, column_sums, False)
            row_out[0, :, pl.ds(first, TILE)] = row_vector(partial)
        return carry

    lax.fori_loop(0, half // TILE, step, 0)
    column_out[0] = jnp.sum(column_sums[...], axis=0, keepdims=True)


def diagonal_totals(own):
    count, depth, columns = own.shape
    pairs = columns * columns // 2
    extended = columns + columns // 2 + TILE
    total = pl.pallas_call(
        diagonal_kernel,
        grid=(count,),
        out_shape=jax.ShapeDtypeStruct((count, 1, columns), jnp.float32),
        in_specs=[pl.BlockSpec((1, depth, columns), lambda w: (w, 0, 0))],
        out_specs=pl.BlockSpec((1, 1, columns), lambda w: (w, 0, 0)),
        scratch_shapes=[
            pltpu.VMEM((depth, extended), own.dtype),
            pltpu.VMEM((SUBLANES, extended), jnp.float32),
        ],
        cost_estimate=pl.CostEstimate(
            flops=count * pairs * 512, bytes_accessed=own.size * 2, transcendentals=0
        ),
    )(own)
    return total.reshape(count, columns)


def cross_totals(tile, own, other):
    count, depth, columns = own.shape
    pairs = columns * columns // 2
    block = pl.BlockSpec((1, depth, columns), lambda w, *_: (w, 0, 0))
    line = pl.BlockSpec((1, 1, columns), lambda w, *_: (w, 0, 0))
    row_part, column_part = pl.pallas_call(
        cross_kernel,
        out_shape=[jax.ShapeDtypeStruct((count, 1, columns), jnp.float32)] * 2,
        grid_spec=pltpu.PrefetchScalarGridSpec(
            num_scalar_prefetch=1,
            grid=(count,),
            in_specs=[block, block],
            out_specs=[line, line],
            scratch_shapes=[pltpu.VMEM((SUBLANES, columns), jnp.float32)],
        ),
        cost_estimate=pl.CostEstimate(
            flops=count * pairs * 512, bytes_accessed=own.size * 4, transcendentals=0
        ),
    )(tile, own, other)
    return row_part.reshape(count, columns), column_part.reshape(count, columns)


def local_windows(tick_bars, prior_bars):
    groups = lax.axis_size("tm")
    group_cols = ASSETS // (2 * groups)
    series = jnp.concatenate(
        [prior_bars.reshape(-1, group_cols), tick_bars.reshape(-1, group_cols)], axis=0
    )
    return window_stack(series)


def shards(tick_bars, prior_bars):
    groups = lax.axis_size("tm")
    outgoing = local_windows(tick_bars, prior_bars)
    arrived = lax.all_to_all(outgoing, "tm", split_axis=0, concat_axis=0, tiled=True)
    arrived = arrived.reshape(groups, WIN_DEV, DEPTH, -1)
    scaled = jnp.transpose(arrived, (1, 2, 0, 3)).reshape(WIN_DEV, DEPTH, -1)
    partner = swapped(scaled, "asset", 0)
    tile = lax.axis_index("asset").astype(jnp.int32).reshape(1)
    diagonal_part = diagonal_totals(scaled)
    row_part, column_part = cross_totals(tile, scaled, partner)
    returned = swapped(column_part.astype(jnp.bfloat16), "asset", 0).astype(jnp.float32)
    totals = diagonal_part + row_part + returned
    return totals * (math.sqrt(SPAN) / ASSETS)


def solution(mesh):
    in_specs = (P("asset", "tm", None), P("asset", "tm", None))
    out_specs = P("tm", "asset")
    return jax.shard_map(shards, mesh=mesh, in_specs=in_specs, out_specs=out_specs, check_vma=False)
```

time: 113 us -> 110 us (0.973)
  matrix products: 45.7 us -> 0 us
  Pallas kernels: 0 us -> 43.6 us
  local copies, waits for them, and re-layouts: 8.66 us -> 6.23 us
  other arithmetic: 8.58 us -> 10.2 us
    dot_general x24 -> x0, matrix products: 45.7 us -> none  [block_magnitude(): lax.dot_general(left_part[:, offset:offset + block_rows], right_part, (((...]
    pallas_call x0 -> x2, Pallas kernels: none -> 43.6 us  [the longest x1 22.2 us: diagonal_totals(): pl.pallas_call(diagonal_kernel, grid=(count,), out_shape=jax.ShapeDtypeSt...]
    dynamic_update_slice x17 -> x0, local copies, waits for them, and re-layouts: 2.34 us -> none  [the longest x12 1.56 us: both_totals(): return lax.map(both_one_window, (own_windows, other_windows))]
    unnamed x3 -> x11, local copies, waits for them, and re-layouts: 0.69 us -> 1.88 us
  transfers between devices with their start and end apart: 2 -> 2, of which waited for: 1 -> 1; matrix products, arithmetic and copies ran while one was open for 27% -> 1% of each run, Pallas kernels for 0% -> 20%
where the time goes in v2:
time: 110 us
  Pallas kernels  43.6 us (40%)
  blocking collectives  27.3 us (25%)
  waiting for transfers between devices  18.9 us (17%)
  other arithmetic  10.2 us (9%)
  local copies, waits for them, and re-layouts  6.23 us (6%)
  starting transfers between devices  3.12 us (3%)
    all_to_all x1, blocking collectives, shards(): lax.all_to_all(outgoing, 'tm', split_axis=0, concat_axis=0, tiled=True)  27.3 us
    pallas_call x1, Pallas kernels, diagonal_totals(): pl.pallas_call(diagonal_kernel, grid=(count,), out_shape=jax.ShapeDtypeSt...  22.2 us
    pallas_call x1, Pallas kernels, cross_totals(): pl.pallas_call(cross_kernel, out_shape=[jax.ShapeDtypeStruct((count, 1, c...  21.4 us
    ppermute x2, waiting for transfers between devices, swapped(): return lax.ppermute(block, axis, route)  18.9 us
    another operation x7, local copies, waits for them, and re-layouts, window_stack(): jnp.stack([groups[offset:offset + count] for offset in range(SPAN // STRI...  4.1 us
    reduce_sum x6, other arithmetic, window_stack(): centred = values - jnp.mean(values, axis=1, keepdims=True)  3.44 us
    ppermute x2, starting transfers between devices, swapped(): return lax.ppermute(block, axis, route)  3.12 us
    unnamed x2, other arithmetic  2.98 us
  transfers between devices with their start and end apart: 2, of which 1 were waited for; matrix products, arithmetic and copies ran while one was open for 1% of the time, Pallas kernels for 20%

profile of v2, /device:TPU:0, one launch (start us, length us, event | category | flops | bytes accessed | tf_op | source)
XLA Modules:
  0.0 109.5 jit_solution(4465341244249251473)
XLA Ops:
  0.0 0.5 broadcast.20
  0.5 2.2 %reduce.14 = f32[61440]{0:T(1024)S(1)} reduce(f32[1,1,61440]{2,1,0:T(1,128)} %param.2, f32[]{:T(128)} %broadcast.20), dimensions={0,1}, to_apply=%param.2.reduce_sub_computation.5 | reduce | bytes 491524 | tf_op args[0]
  2.7 0.1 reshape.53
  2.8 0.8 reduce.8
  3.6 0.8 pad_maximum_fusion
  4.5 0.8 fusion.8
  5.2 0.8 stack.22
  6.0 0.8 stack.23
  6.8 1.0 stack.25
  7.8 1.0 stack.26
  8.8 1.1 %fusion.7 = (f32[48,256]{1,0:T(8,128)S(1)}, f32[48,6,5,256]{3,2,0,1:T(8,128)S(1)}) fusion(f32[48,1,5,256]{3,2,0,1:T(8,128)} %stack.22, f32[48,6,5,256]{3,2,0,1:T(8,128)S(1)} %get-tuple-element.12), kind=kLoop, calls=%fused_computation.28 | loop fusion | flops 49152 | bytes 688128 | tf_op jit(solution)/shard_map/reduce_sum | solution.py:42
  10.0 1.1 %fusion.9 = (f32[48,256]{1,0:T(8,128)S(1)}, f32[48,6,5,256]{3,2,0,1:T(8,128)S(1)}) fusion(f32[48,1,5,256]{3,2,0,1:T(8,128)} %stack.23, f32[48,6,5,256]{3,2,0,1:T(8,128)S(1)} %get-tuple-element.10), kind=kLoop, calls=%fused_computation.30 | loop fusion | flops 49152 | bytes 688128 | tf_op jit(solution)/shard_map/reduce_sum | solution.py:42
  11.1 0.1 fusion.10
  11.3 0.1 fusion.11
  11.4 0.1 fusion.12
  11.6 0.5 copy.8
  12.0 0.2 copy-done.1
  12.2 0.4 multiply_reduce_fusion
  12.6 0.2 fusion.1
  12.8 0.2 copy.13
  13.1 0.1 pad.4.clone
  13.2 27.3 %all_to_all.5 = bf16[48,32,256]{2,1,0:T(8,128)(2,1)S(1)} all-to-all(bf16[48,32,256]{2,1,0:T(8,128)(2,1)S(1)} %pad.4.clone), channel_id=1, replica_groups=mesh['tm'=16,'asset'=2] {'tm'}, dimensions={0} | all-to-all | bytes 1572864 | tf_op jit(solution)/shard_map/all_to_all | solution.py:161
  40.5 0.1 copy.14
  40.6 1.6 %collective-permute-start = (bf16[3,32,4096]{2,1,0:T(8,128)(2,1)S(1)}, bf16[3,32,4096]{2,1,0:T(8,128)(2,1)S(1)}, u32[]{:S(2)}, u32[]{:S(2)}) collective-permute-start(bf16[3,32,4096]{2,1,0:T(8,128)(2,1)S(1)} %bitcast.22), channel_id=1, source_target_pairs={{0,1},{1,0},{2,3},{3,2},{4,5},{5,4},{6,7},{7,6},{8,9},{9,8},{10,11... | collective-permute-start | bytes 2359304 | tf_op jit(solution)/shard_map/ppermute | solution.py:31
  42.1 18.9 %collective-permute-done.other = bf16[3,32,4096]{2,1,0:T(8,128)(2,1)S(1)} collective-permute-done((bf16[3,32,4096]{2,1,0:T(8,128)(2,1)S(1)}, bf16[3,32,4096]{2,1,0:T(8,128)(2,1)S(1)}, u32[]{:S(2)}, u32[]{:S(2)}) %collective-permute-start) | collective-permute-done | bytes 786464 | tf_op jit(solution)/shard_map/ppermute | solution.py:31
  61.0 0.9 copy-done.3
  61.9 21.4 %shard_map.29 = (f32[3,1,4096]{2,1,0:T(1,128)}, f32[3,1,4096]{2,1,0:T(1,128)}) custom-call(s32[1]{0:T(128)} %bitcast.3.tile, bf16[3,32,4096]{2,1,0:T(8,128)(2,1)} %bitcast.23, bf16[3,32,4096]{2,1,0:T(8,128)(2,1)} %copy-done.3), custom_call_target="tpu_custom_call" | custom-call | flops 12884901888 | bytes 1572864 | tf_op jit(solution)/shard_map/pallas_call | solution.py:132
  83.3 0.8 convert_element_type.15
  84.2 1.6 %collective-permute-start.1 = (bf16[3,4096]{1,0:T(4,128)(2,1)S(1)}, bf16[3,4096]{1,0:T(4,128)(2,1)S(1)}, u32[]{:S(2)}, u32[]{:S(2)}) collective-permute-start(bf16[3,4096]{1,0:T(4,128)(2,1)S(1)} %bitcast.25), channel_id=1, source_target_pairs={{0,1},{1,0},{2,3},{3,2},{4,5},{5,4},{6,7},{7,6},{8,9},{9,8},{10,11... | collective-permute-start | bytes 73736 | tf_op jit(solution)/shard_map/ppermute | solution.py:31
  85.8 22.2 %shard_map.28 = f32[3,1,4096]{2,1,0:T(1,128)} custom-call(bf16[3,32,4096]{2,1,0:T(8,128)(2,1)} %bitcast.24), custom_call_target="tpu_custom_call" | custom-call | flops 12884901888 | bytes 786432 | tf_op jit(solution)/shard_map/pallas_call | solution.py:110
  108.0 0.9 add.11
  108.9 0.7 fusion.6
  (13 shorter events, 0.2 us)
Async XLA Ops:
  11.4 0.8 copy-start.1
  40.6 20.4 %copy-start = (bf16[16,3,4,8,256]{4,3,0,2,1:T(8,128)(2,1)}, bf16[16,3,4,8,256]{4,3,0,2,1:T(8,128)(2,1)S(1)}, u32[]{:S(2)}) copy-start(bf16[16,3,4,8,256]{4,3,0,2,1:T(8,128)(2,1)S(1)} %copy.14) | copy-start | bytes 2359300
  40.6 20.4 %collective-permute-start = (bf16[3,32,4096]{2,1,0:T(8,128)(2,1)S(1)}, bf16[3,32,4096]{2,1,0:T(8,128)(2,1)S(1)}, u32[]{:S(2)}, u32[]{:S(2)}) collective-permute-start(bf16[3,32,4096]{2,1,0:T(8,128)(2,1)S(1)} %bitcast.22), channel_id=1, source_target_pairs={{0,1},{1,0},{2,3},{3,2},{4,5},{5,4},{6,7},{7,6},{8,9},{9,8},{10,11... | collective-permute-start | bytes 2359304 | tf_op jit(solution)/shard_map/ppermute | solution.py:31
  61.0 0.9 copy-start.3
  84.2 23.8 %copy-start.2 = (f32[3,1,4096]{2,1,0:T(1,128)S(1)}, f32[3,1,4096]{2,1,0:T(1,128)}, u32[]{:S(2)}) copy-start(f32[3,1,4096]{2,1,0:T(1,128)} %get-tuple-element.7) | copy-start | bytes 147460
  84.2 24.7 %collective-permute-start.1 = (bf16[3,4096]{1,0:T(4,128)(2,1)S(1)}, bf16[3,4096]{1,0:T(4,128)(2,1)S(1)}, u32[]{:S(2)}, u32[]{:S(2)}) collective-permute-start(bf16[3,4096]{1,0:T(4,128)(2,1)S(1)} %bitcast.25), channel_id=1, source_target_pairs={{0,1},{1,0},{2,3},{3,2},{4,5},{5,4},{6,7},{7,6},{8,9},{9,8},{10,11... | collective-permute-start | bytes 73736 | tf_op jit(solution)/shard_map/ppermute | solution.py:31

commit v3 on v1

v3 whole, which is shorter than its diff:
```python
import functools
import math

import jax
import jax.numpy as jnp
from jax import lax
from jax.experimental import pallas as pl
from jax.experimental.pallas import tpu as pltpu
from jax.sharding import PartitionSpec as P

ASSETS = 8192
SPAN = 30
STRIDE = 5
WIN_DEV = 3
LEAD = 25
DEPTH = 32
TILE = 256
LANES = 128
SUBLANES = 8


FLOOR_SQUARES = 1.0


def cycle_next(time, tile):
    core = time % 2
    along = (1 + core + tile) % 2
    return time + along * (1 - 2 * core), tile + (1 - along) * (1 - 2 * tile)


def around(block, forward):
    times, tiles = lax.axis_size("tm"), lax.axis_size("asset")
    route = []
    for time in range(times):
        for tile in range(tiles):
            next_time, next_tile = cycle_next(time, tile)
            hop = (time * tiles + tile, next_time * tiles + next_tile)
            route.append(hop if forward else hop[::-1])
    return lax.ppermute(block, ("tm", "asset"), route)


def window_stack(extended):
    columns = extended.shape[1]
    count = (extended.shape[0] - SPAN) // STRIDE + 1
    groups = extended.reshape(-1, STRIDE, columns)
    stacked = jnp.stack(
        [groups[offset : offset + count] for offset in range(SPAN // STRIDE)], axis=1
    )
    values = stacked.reshape(count, SPAN, columns)
    centred = values - jnp.mean(values, axis=1, keepdims=True)
    squares = jnp.sum(centred * centred, axis=1, keepdims=True)
    scaled = (centred * lax.rsqrt(jnp.maximum(squares, FLOOR_SQUARES))).astype(jnp.bfloat16)
    return jnp.pad(scaled, ((0, 0), (0, DEPTH - SPAN), (0, 0)))


def strip_totals(rows, source, first, count, column_sums, own_first):
    groups, _, width = source.shape
    rows_t = rows.T
    row_partial = jnp.zeros((width, LANES), jnp.float32)
    for offset in range(count):
        group = lax.rem(first + offset, groups)
        magnitude = jnp.abs(jnp.dot(rows_t, source[group], preferred_element_type=jnp.float32))
        for lane in range(0, width, LANES):
            row_partial = row_partial + magnitude[:, lane : lane + LANES]
        if offset or not own_first:
            folded = jnp.sum(magnitude.reshape(width // SUBLANES, SUBLANES, width), axis=0)
            column_sums[group] = column_sums[group] + folded
    return jnp.sum(row_partial.T, axis=0, keepdims=True)


def diagonal(source, out, column_sums):
    groups = source.shape[0]
    half = groups // 2
    column_sums[...] = jnp.zeros_like(column_sums)

    def step(index, carry):
        out[index, 0] = strip_totals(source[index], source, index, half + 1, column_sums, True)
        later = index + half
        out[later, 0] = strip_totals(source[later], source, later, half, column_sums, True)
        return carry

    lax.fori_loop(0, half, step, 0)
    out[:, 0] = out[:, 0] + jnp.sum(column_sums[...], axis=1, keepdims=True)


def totals_kernel(crosses, own, other, own_out, other_out, column_sums):
    groups = own.shape[0]

    @pl.when(crosses[0] == 1)
    def _():
        column_sums[...] = jnp.zeros_like(column_sums)

        def step(index, carry):
            own_out[index, 0] = strip_totals(own[index], other, 0, groups, column_sums, False)
            return carry

        lax.fori_loop(0, groups, step, 0)
        other_out[:, 0] = jnp.sum(column_sums[...], axis=1, keepdims=True)

    @pl.when(crosses[0] == 0)
    def _():
        diagonal(own, own_out, column_sums)
        diagonal(other, other_out, column_sums)


def pair_totals(crosses, own, other):
    groups, depth, width = own.shape
    block = pl.BlockSpec((groups, DEPTH, width), lambda w, *_: (0, w, 0))
    line = pl.BlockSpec((groups, 1, 1, width), lambda w, *_: (0, w, 0, 0))
    return pl.pallas_call(
        totals_kernel,
        out_shape=[jax.ShapeDtypeStruct((groups, depth // DEPTH, 1, width), jnp.float32)] * 2,
        grid_spec=pltpu.PrefetchScalarGridSpec(
            num_scalar_prefetch=1,
            grid=(depth // DEPTH,),
            in_specs=[block, block],
            out_specs=[line, line],
            scratch_shapes=[pltpu.VMEM((groups, SUBLANES, width), jnp.float32)],
        ),
    )(crosses, own, other)


def windows_kernel(tick, prior, out, series):
    width = series.shape[1]
    lead = prior.shape[1] // width
    for row in range(lead):
        series[row : row + 1] = prior[:, row * width : (row + 1) * width]
    for row in range(tick.shape[1] // width):
        series[lead + row : lead + row + 1] = tick[:, row * width : (row + 1) * width]
    for window in range(out.shape[0] * WIN_DEV):
        values = series[window * STRIDE : window * STRIDE + SPAN]
        centred = values - jnp.sum(values, axis=0, keepdims=True) * (1.0 / SPAN)
        squares = jnp.sum(centred * centred, axis=0, keepdims=True)
        scaled = centred * lax.rsqrt(jnp.maximum(squares, FLOOR_SQUARES))
        scaled = jnp.concatenate([scaled, jnp.zeros((DEPTH - SPAN, width), jnp.float32)], axis=0)
        first = window % WIN_DEV * DEPTH
        out[window // WIN_DEV, first : first + DEPTH] = scaled.astype(jnp.bfloat16)


def deliver_kernel(groups, outgoing, own, other, own_send, own_recv, next_send, next_recv, local_sem):
    time = lax.axis_index("tm")
    tile = lax.axis_index("asset")
    next_time, next_tile = cycle_next(time, tile)
    barrier = pltpu.get_barrier_semaphore()
    for step in range(1, groups):
        peer = lax.rem(time + step, groups)
        pl.semaphore_signal(
            barrier, inc=1, device_id=(peer, tile), device_id_type=pl.DeviceIdType.MESH
        )
    pl.semaphore_signal(
        barrier, inc=1, device_id=(time, 1 - tile), device_id_type=pl.DeviceIdType.MESH
    )
    pl.semaphore_wait(barrier, groups)

    def send(step):
        peer = lax.rem(time + step, groups)
        return pltpu.make_async_remote_copy(
            src_ref=outgoing.at[peer],
            dst_ref=own.at[time],
            send_sem=own_send.at[step],
            recv_sem=own_recv.at[step],
            device_id=(peer, tile),
            device_id_type=pl.DeviceIdType.MESH,
        )

    def forward(step):
        source = lax.rem(time - step + groups, groups)
        return pltpu.make_async_remote_copy(
            src_ref=own.at[source],
            dst_ref=other.at[source],
            send_sem=next_send.at[source],
            recv_sem=next_recv.at[source],
            device_id=(next_time, next_tile),
            device_id_type=pl.DeviceIdType.MESH,
        )

    sends = [send(step) for step in range(1, groups)]
    for copy in sends:
        copy.start()
    local = pltpu.make_async_copy(outgoing.at[time], own.at[time], local_sem)
    local.start()
    local.wait()
    forwards = [forward(step) for step in range(groups)]
    forwards[0].start()
    for step in range(1, groups):
        sends[step - 1].wait_recv()
        forwards[step].start()
    for copy in sends:
        copy.wait_send()
    for group in range(groups):
        arrival = pltpu.make_async_remote_copy(
            src_ref=own.at[group],
            dst_ref=other.at[group],
            send_sem=next_send.at[group],
            recv_sem=next_recv.at[group],
            device_id=(next_time, next_tile),
            device_id_type=pl.DeviceIdType.MESH,
        )
        arrival.wait()


def delivered(outgoing):
    groups = outgoing.shape[0]
    vmem = pl.BlockSpec(memory_space=pltpu.VMEM)
    return pl.pallas_call(
        functools.partial(deliver_kernel, groups),
        out_shape=[jax.ShapeDtypeStruct(outgoing.shape, outgoing.dtype)] * 2,
        in_specs=[vmem],
        out_specs=[vmem, vmem],
        scratch_shapes=[pltpu.SemaphoreType.DMA((groups,))] * 4 + [pltpu.SemaphoreType.DMA],
        compiler_params=pltpu.CompilerParams(collective_id=0, has_side_effects=True),
    )(outgoing)


def local_windows(tick_bars, prior_bars):
    groups = lax.axis_size("tm")
    width = ASSETS // (2 * groups)
    ticks, prior = tick_bars.reshape(1, -1), prior_bars.reshape(1, -1)
    if width % LANES:
        series = jnp.concatenate([prior.reshape(-1, width), ticks.reshape(-1, width)], axis=0)
        return window_stack(series).reshape(groups, WIN_DEV * DEPTH, width)
    rows = (ticks.size + prior.size) // width
    return pl.pallas_call(
        windows_kernel,
        out_shape=jax.ShapeDtypeStruct((groups, WIN_DEV * DEPTH, width), jnp.bfloat16),
        scratch_shapes=[pltpu.VMEM((-(-rows // SUBLANES) * SUBLANES, width), jnp.float32)],
    )(ticks, prior)


def retiled(blocks):
    groups, depth, width = blocks.shape
    if width % LANES == 0:
        return blocks
    join = TILE // width
    grouped = blocks.reshape(groups // join, join, depth, width)
    return jnp.transpose(grouped, (0, 2, 1, 3)).reshape(groups // join, depth, TILE)


def shards(tick_bars, prior_bars):
    own, other = delivered(local_windows(tick_bars, prior_bars))
    own, other = retiled(own), retiled(other)
    core = lax.axis_index("tm") % 2
    crosses = (core == lax.axis_index("asset")).astype(jnp.int32).reshape(1)
    own_part, other_part = pair_totals(crosses, own, other)
    own_part = jnp.transpose(own_part[:, :, 0], (1, 0, 2)).reshape(WIN_DEV, -1)
    other_part = jnp.transpose(other_part[:, :, 0], (1, 0, 2)).reshape(WIN_DEV, -1)
    returned = around(other_part.astype(jnp.bfloat16), False).astype(jnp.float32)
    return (own_part + returned) * (math.sqrt(SPAN) / ASSETS)


def solution(mesh):
    in_specs = (P("asset", "tm", None), P("asset", "tm", None))
    out_specs = P("tm", "asset")
    return jax.shard_map(shards, mesh=mesh, in_specs=in_specs, out_specs=out_specs, check_vma=False)
```

time: 113 us -> 79.8 us (0.71)
  the two profiles are of different devices: /device:TPU:0 before, /device:TPU:30 now
where the time goes in v3:
time: 79.8 us; the launch traced here: 79.6 us
  Pallas kernels  74.1 us (93%)
  waiting for transfers between devices  3.12 us (4%)
  other arithmetic  1.49 us (2%)
  local copies, waits for them, and re-layouts  0.81 us (1%)
    pallas_call x1, Pallas kernels, pair_totals(): pl.pallas_call(totals_kernel, out_shape=[jax.ShapeDtypeStruct((groups, de...  42.8 us
    pallas_call x1, Pallas kernels, delivered(): pl.pallas_call(functools.partial(deliver_kernel, groups), out_shape=[jax....  28.4 us
    ppermute x1, waiting for transfers between devices, around(): return lax.ppermute(block, ('tm', 'asset'), route)  3.12 us
    pallas_call x1, Pallas kernels, local_windows(): pl.pallas_call(windows_kernel, out_shape=jax.ShapeDtypeStruct((groups, WI...  2.78 us
  transfers between devices with their start and end apart: 1, of which 1 were waited for; matrix products, arithmetic and copies ran while one was open for 0% of the time, Pallas kernels for 0%

profile of v3, /device:TPU:30, one launch (start us, length us, event | category | flops | bytes accessed | tf_op | source)
XLA Modules:
  0.0 79.6 jit_solution(7809529679203626365)
XLA Ops:
  0.0 2.8 %shard_map.28.outgoing = bf16[16,96,256]{2,1,0:T(8,128)(2,1)} custom-call(f32[1,61440]{1,0:T(1,128)} %bitcast.18, f32[1,6400]{1,0:T(1,128)} %bitcast.22), custom_call_target="tpu_custom_call" | custom-call | tf_op jit(solution)/shard_map/pallas_call | solution.py:223
  2.8 28.4 %shard_map.29 = (bf16[16,96,256]{2,1,0:T(8,128)(2,1)}, bf16[16,96,256]{2,1,0:T(8,128)(2,1)}) custom-call(bf16[16,96,256]{2,1,0:T(8,128)(2,1)} %shard_map.28.outgoing), custom_call_target="tpu_custom_call" | custom-call | tf_op jit(solution)/shard_map/pallas_call | solution.py:205
  31.2 42.8 %shard_map.30 = (f32[16,3,1,256]{3,2,1,0:T(1,128)}, f32[16,3,1,256]{3,2,1,0:T(1,128)}) custom-call(s32[1]{0:T(128)} %bitcast.crosses, bf16[16,96,256]{2,1,0:T(8,128)(2,1)} %get-tuple-element.9.own, bf16[16,96,256]{2,1,0:T(8,128)(2,1)} %get-tuple-element.10.other), custom_call_target="tpu_custom_call" | custom-call | tf_op jit(solution)/shard_map/pallas_call | solution.py:110
  74.1 0.8 %convert_element_type.16 = bf16[16,3,1,256]{3,2,1,0:T(2,128)(2,1)S(1)} convert(f32[16,3,1,256]{3,2,1,0:T(1,128)} %get-tuple-element.12) | non-fusion elementwise | flops 12288 | bytes 73728 | tf_op jit(solution)/shard_map/convert_element_type | solution.py:247
  74.9 0.0 copy-start
  75.0 0.0 collective-permute-start
  75.0 0.7 copy-done
  75.8 3.1 %collective-permute-done = bf16[3,4096]{1,0:T(4,128)(2,1)S(1)} collective-permute-done((bf16[3,4096]{1,0:T(4,128)(2,1)S(1)}, bf16[3,4096]{1,0:T(4,128)(2,1)S(1)}, u32[]{:S(2)}, u32[]{:S(2)}) %collective-permute-start) | collective-permute-done | bytes 24608 | tf_op jit(solution)/shard_map/ppermute | solution.py:39
  78.9 0.7 add_multiply_fusion
  (4 shorter events, 0.1 us)
Async XLA Ops:
  74.9 0.8 %copy-start = (f32[16,3,1,256]{3,2,1,0:T(1,128)S(1)}, f32[16,3,1,256]{3,2,1,0:T(1,128)}, u32[]{:S(2)}) copy-start(f32[16,3,1,256]{3,2,1,0:T(1,128)} %get-tuple-element.11) | copy-start | bytes 147460
  75.0 3.9 %collective-permute-start = (bf16[3,4096]{1,0:T(4,128)(2,1)S(1)}, bf16[3,4096]{1,0:T(4,128)(2,1)S(1)}, u32[]{:S(2)}, u32[]{:S(2)}) collective-permute-start(bf16[3,4096]{1,0:T(4,128)(2,1)S(1)} %bitcast.21), channel_id=1, source_target_pairs={{2,0},{0,1},{3,2},{1,3},{6,4},{4,5},{7,6},{5,7},{10,8},{8,9},{11,1... | collective-permute-start | bytes 73736 | tf_op jit(solution)/shard_map/ppermute | solution.py:39

commit v4 on v3

--- a/solution.py
+++ b/solution.py
@@ -17,6 +17,7 @@
 TILE = 256
 LANES = 128
 SUBLANES = 8
+PART_SCALE = 256.0
 
 
 FLOOR_SQUARES = 1.0
@@ -53,9 +54,21 @@
     return jnp.pad(scaled, ((0, 0), (0, DEPTH - SPAN), (0, 0)))
 
 
+def split_parts(block):
+    scaled = block.astype(jnp.float32) * PART_SCALE
+    high = scaled.astype(jnp.float8_e4m3fn).astype(jnp.float32)
+    return high, scaled - high
+
+
+def right_parts(block):
+    high, low = split_parts(block)
+    return jnp.concatenate([high, high, low, low], axis=0).astype(jnp.float8_e4m3fn)
+
+
 def strip_totals(rows, source, first, count, column_sums, own_first):
     groups, _, width = source.shape
-    rows_t = rows.T
+    high, low = split_parts(rows)
+    rows_t = jnp.concatenate([high, low, high, low], axis=0).T.astype(jnp.float8_e4m3fn)
     row_partial = jnp.zeros((width, LANES), jnp.float32)
     for offset in range(count):
         group = lax.rem(first + offset, groups)
@@ -68,30 +81,40 @@
     return jnp.sum(row_partial.T, axis=0, keepdims=True)
 
 
-def diagonal(source, out, column_sums):
+def fill_parts(source, parts):
+    def fill(group, carry):
+        parts[group] = right_parts(source[group])
+        return carry
+
+    lax.fori_loop(0, source.shape[0], fill, 0)
+
+
+def diagonal(source, out, column_sums, parts):
     groups = source.shape[0]
     half = groups // 2
+    fill_parts(source, parts)
     column_sums[...] = jnp.zeros_like(column_sums)
 
     def step(index, carry):
-        out[index, 0] = strip_totals(source[index], source, index, half + 1, column_sums, True)
+        out[index, 0] = strip_totals(source[index], parts, index, half + 1, column_sums, True)
         later = index + half
-        out[later, 0] = strip_totals(source[later], source, later, half, column_sums, True)
+        out[later, 0] = strip_totals(source[later], parts, later, half, column_sums, True)
         return carry
 
     lax.fori_loop(0, half, step, 0)
     out[:, 0] = out[:, 0] + jnp.sum(column_sums[...], axis=1, keepdims=True)
 
 
-def totals_kernel(crosses, own, other, own_out, other_out, column_sums):
+def totals_kernel(crosses, own, other, own_out, other_out, column_sums, parts):
     groups = own.shape[0]
 
     @pl.when(crosses[0] == 1)
     def _():
+        fill_parts(other, parts)
         column_sums[...] = jnp.zeros_like(column_sums)
 
         def step(index, carry):
-            own_out[index, 0] = strip_totals(own[index], other, 0, groups, column_sums, False)
+            own_out[index, 0] = strip_totals(own[index], parts, 0, groups, column_sums, False)
             return carry
 
         lax.fori_loop(0, groups, step, 0)
@@ -99,8 +122,8 @@
 
     @pl.when(crosses[0] == 0)
     def _():
-        diagonal(own, own_out, column_sums)
-        diagonal(other, other_out, column_sums)
+        diagonal(own, own_out, column_sums, parts)
+        diagonal(other, other_out, column_sums, parts)
 
 
 def pair_totals(crosses, own, other):
@@ -115,7 +138,10 @@
             grid=(depth // DEPTH,),
             in_specs=[block, block],
             out_specs=[line, line],
-            scratch_shapes=[pltpu.VMEM((groups, SUBLANES, width), jnp.float32)],
+            scratch_shapes=[
+                pltpu.VMEM((groups, SUBLANES, width), jnp.float32),
+                pltpu.VMEM((groups, 4 * DEPTH, width), jnp.float8_e4m3fn),
+            ],
         ),
     )(crosses, own, other)
 
@@ -244,8 +270,8 @@
     own_part, other_part = pair_totals(crosses, own, other)
     own_part = jnp.transpose(own_part[:, :, 0], (1, 0, 2)).reshape(WIN_DEV, -1)
     other_part = jnp.transpose(other_part[:, :, 0], (1, 0, 2)).reshape(WIN_DEV, -1)
-    returned = around(other_part.astype(jnp.bfloat16), False).astype(jnp.float32)
-    return (own_part + returned) * (math.sqrt(SPAN) / ASSETS)
+    returned = around(other_part, False)
+    return (own_part + returned) * (math.sqrt(SPAN) / (ASSETS * PART_SCALE * PART_SCALE))
 
 
 def solution(mesh):

time: 79.8 us -> 77.7 us (0.974)
  Pallas kernels: 74.1 us -> 71.7 us
  waiting for transfers between devices: 3.12 us -> 4.21 us
  other arithmetic: 1.49 us -> 0.65 us
    pallas_call x1, Pallas kernels: 42.8 us -> 40.5 us  [pair_totals(): pl.pallas_call(totals_kernel, out_shape=[jax.ShapeDtypeStruct((groups, de...]
    ppermute x1, waiting for transfers between devices: 3.12 us -> 4.21 us  [around(): return lax.ppermute(block, ('tm', 'asset'), route)]
    convert_element_type x1 -> x0, other arithmetic: 0.83 us -> none  [shards(): other_part.astype(jnp.bfloat16)]
where the time goes in v4:
time: 77.7 us; the launch traced here: 77.5 us
  Pallas kernels  71.7 us (92%)
  waiting for transfers between devices  4.21 us (5%)
  local copies, waits for them, and re-layouts  0.9 us (1%)
    pallas_call x1, Pallas kernels, pair_totals(): pl.pallas_call(totals_kernel, out_shape=[jax.ShapeDtypeStruct((groups, de...  40.5 us
    pallas_call x1, Pallas kernels, delivered(): pl.pallas_call(functools.partial(deliver_kernel, groups), out_shape=[jax....  28.4 us
    ppermute x1, waiting for transfers between devices, around(): return lax.ppermute(block, ('tm', 'asset'), route)  4.21 us
    pallas_call x1, Pallas kernels, local_windows(): pl.pallas_call(windows_kernel, out_shape=jax.ShapeDtypeStruct((groups, WI...  2.78 us
  transfers between devices with their start and end apart: 1, of which 1 were waited for; matrix products, arithmetic and copies ran while one was open for 0% of the time, Pallas kernels for 0%

profile of v4, /device:TPU:30, one launch (start us, length us, event | category | flops | bytes accessed | tf_op | source)
XLA Modules:
  0.0 77.5 jit_solution(5136868132278588554)
XLA Ops:
  0.0 2.8 %shard_map.28.outgoing = bf16[16,96,256]{2,1,0:T(8,128)(2,1)} custom-call(f32[1,61440]{1,0:T(1,128)} %bitcast.16, f32[1,6400]{1,0:T(1,128)} %bitcast.18), custom_call_target="tpu_custom_call" | custom-call | tf_op jit(solution)/shard_map/pallas_call | solution.py:249
  2.8 28.4 %shard_map.29 = (bf16[16,96,256]{2,1,0:T(8,128)(2,1)}, bf16[16,96,256]{2,1,0:T(8,128)(2,1)}) custom-call(bf16[16,96,256]{2,1,0:T(8,128)(2,1)} %shard_map.28.outgoing), custom_call_target="tpu_custom_call" | custom-call | tf_op jit(solution)/shard_map/pallas_call | solution.py:231
  31.2 40.5 %shard_map.30 = (f32[16,3,1,256]{3,2,1,0:T(1,128)}, f32[16,3,1,256]{3,2,1,0:T(1,128)}) custom-call(s32[1]{0:T(128)} %bitcast.crosses, bf16[16,96,256]{2,1,0:T(8,128)(2,1)} %get-tuple-element.9.own, bf16[16,96,256]{2,1,0:T(8,128)(2,1)} %get-tuple-element.10.other), custom_call_target="tpu_custom_call" | custom-call | tf_op jit(solution)/shard_map/pallas_call | solution.py:133
  71.7 0.8 %copy_bitcast_fusion = (f32[1,3,16,256]{3,2,1,0:T(8,128)S(1)}, f32[1,3,16,256]{3,2,1,0:T(8,128)S(1)}) fusion(f32[16,3,1,256]{3,2,1,0:T(1,128)} %get-tuple-element.12, f32[16,3,1,256]{3,2,1,0:T(1,128)} %get-tuple-element.11), kind=kLoop, calls=%fused_computation.1 | loop fusion | bytes 196608
  72.6 0.0 collective-permute-start
  72.6 4.2 %collective-permute-done = f32[3,4096]{1,0:T(4,128)S(1)} collective-permute-done((f32[3,4096]{1,0:T(4,128)S(1)}, f32[3,4096]{1,0:T(4,128)S(1)}, u32[]{:S(2)}, u32[]{:S(2)}) %collective-permute-start) | collective-permute-done | bytes 49184 | tf_op jit(solution)/shard_map/ppermute | solution.py:40
  76.8 0.7 add_multiply_fusion
  (2 shorter events, 0.1 us)
Async XLA Ops:
  72.6 4.3 %collective-permute-start = (f32[3,4096]{1,0:T(4,128)S(1)}, f32[3,4096]{1,0:T(4,128)S(1)}, u32[]{:S(2)}, u32[]{:S(2)}) collective-permute-start(f32[3,4096]{1,0:T(4,128)S(1)} %bitcast.17), channel_id=1, source_target_pairs={{2,0},{0,1},{3,2},{1,3},{6,4},{4,5},{7,6},{5,7},{10,8},{8,9},{11,1... | collective-permute-start | bytes 147464 | tf_op jit(solution)/shard_map/ppermute | solution.py:40
